TPU v7x, 128 devices: a whole 4x4x4 slice. The times are simulated.
128 devices in a mesh: dp: 64 (over z, y, x), mp: 2 (over core).
Axes of the slice: x: 4, y: 4, z: 4, core: 2. Of those that a mesh axis runs over, the one named last changes fastest.
Arguments:
- hot_rows: int32 [64, 64, 32], P('dp'), may hold values from 0 to 4095
- hot_count: int32 [64, 64], P('dp'), may hold values from 1 to 32, as said below
- hot_cot: bfloat16 [64, 64, 32, 128], P('dp'), may hold values from -6 to 6
- table: float32 [262144, 128], P('dp'), may hold values from -3 to 3
- cold_ids: int32 [65536], P('dp'), may hold values from 0 to 1048575
- hash_mult: int32 [1024], replicated, may hold values from 1 to 1023
- hash_add: int32 [1024], replicated, may hold values from 0 to 1000002
- layer_one: bfloat16 [1024, 1024], P(None, 'mp'), may hold values from -0.1875 to 0.1875
- layer_two: bfloat16 [1024, 1024], P('mp'), may hold values from -0.1875 to 0.1875
- layer_three: bfloat16 [1024, 1024], P(None, 'mp'), may hold values from -0.1875 to 0.1875
- layer_four: bfloat16 [1024, 128], P('mp'), may hold values from -0.1875 to 0.1875
- cold_cot: bfloat16 [65536, 128], P('dp'), may hold values from -6 to 6
Outputs:
- hot_emb: bfloat16 [64, 64, 32, 128], P('dp')
- new_table: float32 [262144, 128], P('dp')
- cold_emb: bfloat16 [65536, 128], P('dp')
- grad_one: float32 [1024, 1024], P(None, 'mp')
- grad_two: float32 [1024, 1024], P('mp')
- grad_three: float32 [1024, 1024], P(None, 'mp')
- grad_four: float32 [1024, 128], P('mp')
Inputs may be any that keep to these rules, and one draw needn't show every extreme that they name: `hot_rows`: entries index the owner's block of 4096 rows; entries in unused slots are arbitrary. `hot_count`: every batch shard fills all 32 slots of some owner, and some owner receives 32 from every batch shard.
All inputs are finite; a program needn't handle non-finite values.
Results may differ from a plain program's by a relative error of at most 0.0074.
Values may be sent and summed in bfloat16 or wider, within the bound.
A program may use at most 128 MiB of HBM per device.

v0:
```python
import jax
import jax.numpy as jnp
from jax import lax
from jax.sharding import PartitionSpec as P

COLD = 1024
learn_rate = 0.5
modulus = 1000003


def over_pieces(array, axis):
    return lax.all_gather(array, axis).sum(0)


def from_everyone(array, axis):
    size = lax.axis_size(axis)
    return lax.all_to_all(
        jnp.broadcast_to(array[None], (size, *array.shape)), axis, 0, 0, tiled=True
    )


def over_copies(array, axis):
    everything = from_everyone(array, axis)
    return jnp.sum(everything, axis=0)


def in_order(tiles, dim):
    dims = list(tiles.shape[1:])
    dims[dim] *= tiles.shape[0]
    return jnp.moveaxis(tiles, 0, dim).reshape(dims)


def gather_directly(array, axis, dim):
    return in_order(from_everyone(array, axis), dim)


def features_of(ids, hash_mult, hash_add):
    hashed = jnp.remainder(ids[:, None] * hash_mult[None, :] + hash_add[None, :], modulus)
    return (hashed.astype(jnp.float32) * (2.0 / 1000002.0) - 1.0).astype(jnp.bfloat16)


def silu_grad(value):
    sig = jax.nn.sigmoid(value)
    return sig * (1.0 + value * (1.0 - sig))


def local(
    hot_rows,
    hot_count,
    hot_cot,
    table,
    cold_ids,
    hash_mult,
    hash_add,
    layer_one,
    layer_two,
    layer_three,
    layer_four,
    cold_cot,
):
    width = table.shape[1]
    slots_all = hot_rows.shape[2]
    span = slots_all // lax.axis_size("mp")
    begin = lax.axis_index("mp") * span
    mine = lax.dynamic_slice_in_dim(hot_rows, begin, span, 2)
    received = lax.all_to_all(mine, "dp", split_axis=1, concat_axis=1, tiled=True)
    fetched = jnp.take(table, received.reshape(-1), axis=0).astype(jnp.bfloat16)
    fetched = fetched.reshape(received.shape + (width,))
    returned = lax.all_to_all(fetched, "dp", split_axis=1, concat_axis=1, tiled=True)
    returned, received = (returned, received)
    feats = features_of(cold_ids, hash_mult, hash_add)
    pre_one = jnp.dot(feats, layer_one, preferred_element_type=jnp.float32)
    act_one = jax.nn.silu(pre_one).astype(jnp.bfloat16)
    pre_two = over_pieces(jnp.dot(act_one, layer_two, preferred_element_type=jnp.float32), "mp")
    act_two = jax.nn.silu(pre_two).astype(jnp.bfloat16)
    pre_three = jnp.dot(act_two, layer_three, preferred_element_type=jnp.float32)
    act_three = jax.nn.silu(pre_three).astype(jnp.bfloat16)
    cold_emb = over_copies(
        jnp.dot(act_three, layer_four, preferred_element_type=jnp.float32), "mp"
    ).astype(jnp.bfloat16)
    slot_index = begin + jnp.arange(span, dtype=jnp.int32)
    used = slot_index[None, None, :] < hot_count[:, :, None]
    own_emb = jnp.where(used[..., None], returned, jnp.zeros_like(returned))
    own_cot = lax.dynamic_slice_in_dim(hot_cot, begin, span, 2)
    own_cot = jnp.where(used[..., None], own_cot, jnp.zeros_like(own_cot))
    arrived = lax.all_to_all(own_cot, "dp", split_axis=1, concat_axis=1, tiled=True)
    factor = float(COLD * lax.axis_size("dp")) ** (-0.5)
    back_three = (
        jnp.dot(cold_cot, layer_four.T, preferred_element_type=jnp.float32) * silu_grad(pre_three)
    ).astype(jnp.bfloat16)
    part_four = jnp.dot(act_three.T, cold_cot, preferred_element_type=jnp.float32) * factor
    back_sum = over_pieces(
        jnp.dot(back_three, layer_three.T, preferred_element_type=jnp.float32), "mp"
    )
    part_three = jnp.dot(act_two.T, back_three, preferred_element_type=jnp.float32) * factor
    back_two = (back_sum * silu_grad(pre_two)).astype(jnp.bfloat16)
    part_two = jnp.dot(act_one.T, back_two, preferred_element_type=jnp.float32) * factor
    back_one = (
        jnp.dot(back_two, layer_two.T, preferred_element_type=jnp.float32) * silu_grad(pre_one)
    ).astype(jnp.bfloat16)
    part_one = jnp.dot(feats.T, back_one, preferred_element_type=jnp.float32) * factor
    part_one, part_two, part_three, part_four = lax.psum(
        (part_one, part_two, part_three, part_four), "dp"
    )
    arrived = gather_directly(arrived, "mp", 2)
    received = gather_directly(received, "mp", 2)
    hot_emb = gather_directly(own_emb, "mp", 2)
    delta = (
        jnp.zeros_like(table)
        .at[received.reshape(-1)]
        .add(arrived.reshape(-1, width).astype(jnp.float32))
    )
    new_table = table - learn_rate * delta
    return (hot_emb, new_table, cold_emb, part_one, part_two, part_three, part_four)


def solution(mesh):
    in_specs = (
        P("dp", None, None),
        P("dp", None),
        P("dp", None, None, None),
        P("dp", None),
        P("dp"),
        P(),
        P(),
        P(None, "mp"),
        P("mp", None),
        P(None, "mp"),
        P("mp", None),
        P("dp", None),
    )
    out_specs = (
        P("dp", None, None, None),
        P("dp", None),
        P("dp", None),
        P(None, "mp"),
        P("mp", None),
        P(None, "mp"),
        P("mp", None),
    )
    return jax.shard_map(local, mesh=mesh, in_specs=in_specs, out_specs=out_specs, check_vma=False)
```

profile of v0, /device:TPU:1, one launch (start us, length us, event | category | flops | bytes accessed | tf_op | source)
XLA Modules:
  0.0 269.9 jit_solution(9633521886486711486)
XLA Ops:
  7.2 0.0 copy-start
  7.2 0.0 all-gather.5.cloned.1.call-start
  7.2 4.8 %fusion.9 = f32[1024,512]{1,0:T(8,128)S(1)} fusion(bf16[1024,512]{1,0:T(8,128)(2,1)} %param.19, s32[1024]{0:T(1024)} %param.18, s32[1024]{0:T(1024)} %param.17, s32[1024]{0:T(1024)} %param.16), kind=kOutput, calls=%fused_computation.21 | convolution fusion | flops 1086324736 | bytes 3158016 | tf_op jit(solution)/shard_map/dot_general | solution.py:72
  12.0 1.3 copy-done.19
  13.4 3.3 %fusion.25 = f32[1024,1024]{1,0:T(8,128)} fusion(bf16[512,1024]{1,0:T(8,128)(2,1)S(1)} %copy-done.14, f32[1024,512]{1,0:T(8,128)S(1)} %fusion.9), kind=kOutput, calls=%fused_computation.50 | convolution fusion | flops 1076363264 | bytes 7340032 | tf_op jit(solution)/shard_map/dot_general | solution.py:74
  16.6 0.0 all-gather.5.cloned.1.call-update
  16.6 0.0 all-gather.7.cloned.1.call-start
  16.7 26.3 %all-gather.5.cloned.1.call-done = f32[2048,1024]{1,0:T(8,128)} async-done(((f32[1024,1024]{1,0:T(8,128)}), f32[2048,1024]{1,0:T(8,128)}) %all-gather.5.cloned.1.call-update) | async-done | bytes 8388624 | tf_op jit(solution)/shard_map/all_gather | solution.py:12
  43.0 6.7 %reduce_sum.27 = f32[1024,1024]{1,0:T(8,128)} reduce(f32[2,1024,1024]{2,1,0:T(8,128)} %bitcast.44, f32[]{:T(128)} %constant.31.clone.1), dimensions={0}, to_apply=%region_1.2 | reduce | flops 1048576 | bytes 12582916 | tf_op jit(solution)/shard_map/reduce_sum | solution.py:12
  49.6 3.3 %multiply_convert_fusion.1 = bf16[1024,1024]{1,0:T(8,128)(2,1)S(1)} fusion(f32[1024,1024]{1,0:T(8,128)} %reduce_sum.27), kind=kLoop, calls=%fused_computation.8 | loop fusion | flops 5242880 | bytes 6291456 | tf_op jit(solution)/shard_map/convert_element_type | solution.py:75
  53.0 1.5 multiply_convert_fusion.4
  54.6 0.9 multiply_convert_fusion.3
  55.4 3.2 %fusion.27 = f32[1024,1024]{1,0:T(8,128)} fusion(bf16[1024,512]{1,0:T(8,128)(2,1)S(1)} %multiply_convert_fusion.3, bf16[1024,512]{1,0:T(8,128)(2,1)S(1)} %copy-done), kind=kOutput, calls=%fused_computation.54 | convolution fusion | flops 1073741824 | bytes 6291456 | tf_op jit(solution)/shard_map/dot_general | solution.py:93
  58.7 0.0 all-gather.7.cloned.1.call-update
  58.7 0.2 all-reduce.3.cloned.1.call-start
  58.9 1.2 convolution_multiply_fusion.2
  60.1 4.2 %convolution_multiply_fusion = f32[1024,512]{1,0:T(8,128)} fusion(bf16[1024,1024]{1,0:T(8,128)(2,1)} %copy-done.5, bf16[1024,512]{1,0:T(8,128)(2,1)S(1)} %multiply_convert_fusion.3), kind=kOutput, calls=%fused_computation.23 | convolution fusion | flops 1074266112 | bytes 5242880 | tf_op jit(solution)/shard_map/dot_general | solution.py:95
  64.3 18.4 %all-gather.7.cloned.1.call-done = f32[2048,1024]{1,0:T(8,128)} async-done(((f32[1024,1024]{1,0:T(8,128)}), f32[2048,1024]{1,0:T(8,128)}) %all-gather.7.cloned.1.call-update) | async-done | bytes 8388624 | tf_op jit(solution)/shard_map/all_gather | solution.py:12
  82.8 6.6 %reduce_sum.29 = f32[1024,1024]{1,0:T(8,128)} reduce(f32[2,1024,1024]{2,1,0:T(8,128)} %bitcast.43, f32[]{:T(128)} %constant.31.clone.1), dimensions={0}, to_apply=%region_3.4 | reduce | flops 1048576 | bytes 12582916 | tf_op jit(solution)/shard_map/reduce_sum | solution.py:12
  89.4 5.0 %multiply_convert_fusion = bf16[1024,1024]{1,0:T(8,128)(2,1)S(1)} fusion(f32[1024,1024]{1,0:T(8,128)} %reduce_sum.29, f32[1024,1024]{1,0:T(8,128)} %reduce_sum.27), kind=kLoop, calls=%fused_computation.7 | loop fusion | flops 9437184 | bytes 10485760 | tf_op jit(solution)/shard_map/convert_element_type | solution.py:96
  94.5 2.6 convolution_multiply_fusion.1
  97.2 8.1 %fusion.11 = f32[1024,512]{1,0:T(8,128)} fusion(s32[1024]{0:T(1024)S(1)} %copy-done.16, s32[1024]{0:T(1024)S(1)} %copy-done.17, s32[1024]{0:T(1024)S(1)} %copy-done.18, f32[1024,512]{1,0:T(8,128)} %copy-done.19, bf16[1024,1024]{1,0:T(8,128)(2,1)S(1)} %multiply_convert_fusion, bf16[512,1024]{1,0:T(8,128)(2,1)S(1)} %copy-done.15), kind=kOutput, calls=%fused_computation.25 | convolution fusion | flops 2165309440 | bytes 7352320 | tf_op jit(solution)/shard_map/dot_general | solution.py:101
  105.3 0.0 all-reduce.3.cloned.1.call-update
  105.4 0.7 copy-done.12
  106.0 0.7 copy.43
  106.7 10.1 %all-to-all-start = ((s32[1,64,16]{2,0,1:T(1,128)}), s32[1,64,16]{2,0,1:T(1,128)S(1)}, u32[]{:S(2)}, u32[]{:S(2)}) async-start(s32[1,64,16]{2,0,1:T(1,128)} %copy.43), calls=%async_computation | async-start | bytes 65536 | tf_op jit(solution)/shard_map/all_to_all | solution.py:66
  116.8 8.7 %all-to-all-done = s32[1,64,16]{2,0,1:T(1,128)S(1)} async-done(((s32[1,64,16]{2,0,1:T(1,128)}), s32[1,64,16]{2,0,1:T(1,128)S(1)}, u32[]{:S(2)}, u32[]{:S(2)}) %all-to-all-start) | async-done | bytes 4128 | tf_op jit(solution)/shard_map/all_to_all | solution.py:66
  125.5 0.1 copy.39
  125.6 0.7 reshape.200
  126.3 4.9 %all-to-all-start.3 = ((s32[2,1,1024]{2,1,0:T(1,128)}), s32[2,1,1024]{2,1,0:T(1,128)S(1)}, u32[]{:S(2)}, u32[]{:S(2)}) async-start(s32[2,1,1024]{2,1,0:T(1,128)} %reshape.200), calls=%async_computation.3 | async-start | bytes 16384 | tf_op jit(solution)/shard_map/all_to_all | solution.py:17
  131.1 0.5 broadcast.139
  131.7 0.7 reduce.3
  132.4 0.1 reshape.168
  132.5 2.9 %gather_fusion = bf16[1024,128]{1,0:T(8,128)(2,1)S(1)} fusion(f32[4096,128]{1,0:T(8,128)S(1)} %copy-done.2, s32[1024]{0:T(1024)S(1)} %broadcast_clamp_fusion), kind=kCustom, calls=%fused_computation | custom fusion | bytes 528384 | tf_op jit(solution)/shard_map/jit(_take)/gather | solution.py:67
  135.4 0.9 select_convert_fusion
  136.3 4.6 %all-to-all-start.1 = ((bf16[1,64,16,128]{3,2,0,1:T(8,128)(2,1)}), bf16[1,64,16,128]{3,2,0,1:T(8,128)(2,1)S(1)}, u32[]{:S(2)}, u32[]{:S(2)}) async-start(bf16[1,64,16,128]{3,2,0,1:T(8,128)(2,1)} %select_convert_fusion), calls=%async_computation.1 | async-start | bytes 524288 | tf_op jit(solution)/shard_map/all_to_all | solution.py:69
  141.0 0.1 broadcast_compare_fusion
  141.1 0.5 broadcast.140
  141.6 0.7 reduce.4
  142.3 0.1 reshape.201
  142.4 0.1 copy.40
  142.5 0.1 reshape_reshape.4
  142.6 8.5 %all-to-all-done.1 = bf16[1,64,16,128]{3,2,0,1:T(8,128)(2,1)S(1)} async-done(((bf16[1,64,16,128]{3,2,0,1:T(8,128)(2,1)}), bf16[1,64,16,128]{3,2,0,1:T(8,128)(2,1)S(1)}, u32[]{:S(2)}, u32[]{:S(2)}) %all-to-all-start.1) | async-done | bytes 262176 | tf_op jit(solution)/shard_map/all_to_all | solution.py:69
  151.1 0.9 dynamic-slice_select_fusion
  152.0 0.1 broadcast_in_dim.64
  152.1 5.2 %all_to_all.35 = bf16[2,1,64,16,128]{4,3,2,1,0:T(8,128)(2,1)S(1)} all-to-all(bf16[2,1,64,16,128]{4,3,2,1,0:T(8,128)(2,1)S(1)} %broadcast_in_dim.64), channel_id=1, replica_groups=mesh['dp'=64,'mp'=2] {'mp'}, dimensions={0} | all-to-all | bytes 1048576 | tf_op jit(solution)/shard_map/all_to_all | solution.py:17
  157.3 4.6 %all-to-all-start.4 = ((bf16[1,64,16,128]{3,2,0,1:T(8,128)(2,1)}), bf16[1,64,16,128]{3,2,0,1:T(8,128)(2,1)S(1)}, u32[]{:S(2)}, u32[]{:S(2)}) async-start(bf16[1,64,16,128]{3,2,0,1:T(8,128)(2,1)} %get-tuple-element.11), calls=%async_computation.4 | async-start | bytes 524288 | tf_op jit(solution)/shard_map/all_to_all | solution.py:86
  162.0 0.8 copy.38
  162.8 9.2 %all-to-all-done.4 = bf16[1,64,16,128]{3,2,0,1:T(8,128)(2,1)S(1)} async-done(((bf16[1,64,16,128]{3,2,0,1:T(8,128)(2,1)}), bf16[1,64,16,128]{3,2,0,1:T(8,128)(2,1)S(1)}, u32[]{:S(2)}, u32[]{:S(2)}) %all-to-all-start.4) | async-done | bytes 262176 | tf_op jit(solution)/shard_map/all_to_all | solution.py:86
  172.0 0.1 broadcast_in_dim.68
  172.1 5.3 %all_to_all.36 = bf16[2,1,64,16,128]{4,3,2,1,0:T(8,128)(2,1)S(1)} all-to-all(bf16[2,1,64,16,128]{4,3,2,1,0:T(8,128)(2,1)S(1)} %broadcast_in_dim.68), channel_id=1, replica_groups=mesh['dp'=64,'mp'=2] {'mp'}, dimensions={0} | all-to-all | bytes 1048576 | tf_op jit(solution)/shard_map/all_to_all | solution.py:17
  177.3 1.1 copy_convert_fusion
  178.5 13.2 %scatter_custom_fusion = f32[4096,128]{1,0:T(8,128)} fusion(s32[2048]{0:T(1024)S(1)} %bitcast.53, f32[2048,128]{1,0:T(8,128)} %bitcast.47, f32[]{:T(128)} %constant.31.clone.1), kind=kCustom, calls=%fused_computation.27 | custom fusion | flops 262144 | bytes 2097664 | tf_op jit(solution)/shard_map/scatter-add | solution.py:111
  191.7 3.2 %multiply_subtract_fusion = f32[4096,128]{1,0:T(8,128)} fusion(f32[4096,128]{1,0:T(8,128)S(1)} %copy-done.2, f32[4096,128]{1,0:T(8,128)} %scatter_custom_fusion), kind=kLoop, calls=%fused_computation.22 | loop fusion | flops 1048576 | bytes 6291456 | tf_op jit(solution)/shard_map/sub | solution.py:113
  194.9 0.4 fusion.26
  195.3 0.1 broadcast_in_dim.69
  195.4 4.6 %all_to_all.37 = f32[2,1024,128]{2,1,0:T(8,128)S(1)} all-to-all(f32[2,1024,128]{2,1,0:T(8,128)S(1)} %broadcast_in_dim.69), channel_id=1, replica_groups=mesh['dp'=64,'mp'=2] {'mp'}, dimensions={0} | all-to-all | bytes 2097152 | tf_op jit(solution)/shard_map/all_to_all | solution.py:17
  200.0 0.8 reduce_sum.28
  200.8 54.9 %all-reduce.3.cloned.1.call-done = (f32[1024,512]{1,0:T(8,128)}, f32[512,1024]{1,0:T(8,128)}, f32[1024,512]{1,0:T(8,128)}, f32[512,128]{1,0:T(8,128)}) async-done(((f32[1024,512]{1,0:T(8,128)}, f32[512,1024]{1,0:T(8,128)}, f32[1024,512]{1,0:T(8,128)}, f32[512,128]{1,0:T(8,128)}), (f32[1024,512]{1,0:T(8,128)}, f32[512,1024]{1,0:T(8,128)}, f32[1024,512]{1,0:T(8,128)}, ...) | async-done | bytes 6553616 | tf_op jit(solution)/shard_map/psum | solution.py:102
  255.7 3.2 %copy.49 = f32[1024,512]{1,0:T(8,128)} copy(f32[1024,512]{1,0:T(8,128)} %get-tuple-element.18) | data formatting | bytes 4194304
  259.0 1.3 copy.50
  260.3 1.0 copy-done.6
  261.3 1.3 copy.51
  262.6 0.7 copy.52
  (47 shorter events, 0.2 us)
Async XLA Ops:
  7.2 45.8 %copy-start = (bf16[1024,512]{1,0:T(8,128)(2,1)S(1)}, bf16[1024,512]{1,0:T(8,128)(2,1)}, u32[]{:S(2)}) copy-start(bf16[1024,512]{1,0:T(8,128)(2,1)} %param.21) | copy-start | bytes 3145732
  7.2 6.2 %copy-start.14 = (bf16[512,1024]{1,0:T(8,128)(2,1)S(1)}, bf16[512,1024]{1,0:T(8,128)(2,1)}, u32[]{:S(2)}) copy-start(bf16[512,1024]{1,0:T(8,128)(2,1)} %param.20) | copy-start | bytes 3145732
  7.2 35.8 %all-gather.5.cloned.1.call-start = ((), (), s32[]{:S(2)}) async-start(), calls=%async_computation.7 | async-start | bytes 12582912 | tf_op jit(solution)/shard_map/all_gather | solution.py:12
  12.0 1.3 copy-start.19
  16.6 66.1 %all-gather.7.cloned.1.call-start = ((), (), s32[]{:S(2)}) async-start(), calls=%async_computation.8 | async-start | bytes 12582912 | tf_op jit(solution)/shard_map/all_gather | solution.py:12
  53.0 1.6 copy-start.5
  53.0 1.6 copy-start.9
  53.0 1.6 copy-start.11
  54.5 4.4 %copy-start.3 = (bf16[1024,512]{1,0:T(8,128)(2,1)}, bf16[1024,512]{1,0:T(8,128)(2,1)S(1)}, u32[]{:S(2)}) copy-start(bf16[1024,512]{1,0:T(8,128)(2,1)S(1)} %get-tuple-element.13) | copy-start | bytes 3145732
  58.7 197.0 %all-reduce.3.cloned.1.call-start = ((), (), s32[]{:S(2)}) async-start(), calls=%async_computation.9 | async-start | bytes 13107200 | tf_op jit(solution)/shard_map/psum | solution.py:102
  89.4 5.1 %copy-start.20 = (f32[1024,512]{1,0:T(8,128)S(1)}, f32[1024,512]{1,0:T(8,128)}, u32[]{:S(2)}) copy-start(f32[1024,512]{1,0:T(8,128)} %copy-done.19) | copy-start | bytes 6291460
  94.5 2.7 copy-start.15
  94.5 2.7 copy-start.16
  94.5 2.7 copy-start.17
  94.5 2.7 copy-start.18
  105.3 0.7 copy-start.12
  105.3 27.2 %copy-start.2 = (f32[4096,128]{1,0:T(8,128)S(1)}, f32[4096,128]{1,0:T(8,128)}, u32[]{:S(2)}) copy-start(f32[4096,128]{1,0:T(8,128)} %param.15) | copy-start | bytes 6291460
  105.3 35.7 %copy-start.13 = (s32[1,64]{1,0:T(1,128)S(1)}, s32[1,64]{1,0:T(1,128)}, u32[]{:S(2)}) copy-start(s32[1,64]{1,0:T(1,128)} %param.13) | copy-start | bytes 772
  105.3 45.8 %copy-start.10 = (bf16[1,64,32,128]{3,2,1,0:T(8,128)(2,1)S(1)}, bf16[1,64,32,128]{3,2,1,0:T(8,128)(2,1)}, u32[]{:S(2)}) copy-start(bf16[1,64,32,128]{3,2,1,0:T(8,128)(2,1)} %param.14) | copy-start | bytes 1572868
  106.7 18.8 %all-to-all-start = ((s32[1,64,16]{2,0,1:T(1,128)}), s32[1,64,16]{2,0,1:T(1,128)S(1)}, u32[]{:S(2)}, u32[]{:S(2)}) async-start(s32[1,64,16]{2,0,1:T(1,128)} %copy.43), calls=%async_computation | async-start | bytes 65536 | tf_op jit(solution)/shard_map/all_to_all | solution.py:66
  126.3 10.1 %all-to-all-start.3 = ((s32[2,1,1024]{2,1,0:T(1,128)}), s32[2,1,1024]{2,1,0:T(1,128)S(1)}, u32[]{:S(2)}, u32[]{:S(2)}) async-start(s32[2,1,1024]{2,1,0:T(1,128)} %reshape.200), calls=%async_computation.3 | async-start | bytes 16384 | tf_op jit(solution)/shard_map/all_to_all | solution.py:17
  136.3 14.8 %all-to-all-start.1 = ((bf16[1,64,16,128]{3,2,0,1:T(8,128)(2,1)}), bf16[1,64,16,128]{3,2,0,1:T(8,128)(2,1)S(1)}, u32[]{:S(2)}, u32[]{:S(2)}) async-start(bf16[1,64,16,128]{3,2,0,1:T(8,128)(2,1)} %select_convert_fusion), calls=%async_computation.1 | async-start | bytes 524288 | tf_op jit(solution)/shard_map/all_to_all | solution.py:69
  157.3 14.7 %all-to-all-start.4 = ((bf16[1,64,16,128]{3,2,0,1:T(8,128)(2,1)}), bf16[1,64,16,128]{3,2,0,1:T(8,128)(2,1)S(1)}, u32[]{:S(2)}, u32[]{:S(2)}) async-start(bf16[1,64,16,128]{3,2,0,1:T(8,128)(2,1)} %get-tuple-element.11), calls=%async_computation.4 | async-start | bytes 524288 | tf_op jit(solution)/shard_map/all_to_all | solution.py:86
  191.7 3.2 %copy-start.4 = (bf16[1024,512]{1,0:T(8,128)(2,1)S(1)}, bf16[1024,512]{1,0:T(8,128)(2,1)}, u32[]{:S(2)}) copy-start(bf16[1024,512]{1,0:T(8,128)(2,1)} %copy-done.3) | copy-start | bytes 3145732
  255.7 3.2 %copy-start.7 = (f32[512,1024]{1,0:T(8,128)S(1)}, f32[512,1024]{1,0:T(8,128)}, u32[]{:S(2)}) copy-start(f32[512,1024]{1,0:T(8,128)} %get-tuple-element.19) | copy-start | bytes 6291460
  259.0 2.3 copy-start.6
  259.0 4.4 %copy-start.1 = (bf16[1024,512]{1,0:T(8,128)(2,1)S(1)}, bf16[1024,512]{1,0:T(8,128)(2,1)}, u32[]{:S(2)}) copy-start(bf16[1024,512]{1,0:T(8,128)(2,1)} %param.21) | copy-start | bytes 3145732
  261.3 1.3 copy-start.8
Sparse Core Ops, SparseCore 0:
  16.8 26.1 all-gather.4
  58.8 23.8 all-gather.6
  105.5 150.2 all-reduce.2
where the time goes:
time: 271 us; the launch traced here: 270 us
  waiting for transfers between devices  126 us (46%)
  other arithmetic  43.4 us (16%)
  matrix products  30.2 us (11%)
  starting transfers between devices  24.6 us (9%)
  local copies, waits for them, and re-layouts  16.5 us (6%)
  blocking collectives  15.1 us (6%)
  between operations  14.1 us (5%)
    psum x1, waiting for transfers between devices, local(): lax.psum((part_one, part_two, part_three, part_four), 'dp')  54.9 us
    all_gather x2, waiting for transfers between devices, over_pieces(): return lax.all_gather(array, axis).sum(0)  44.7 us
    all_to_all x3, blocking collectives, from_everyone(): lax.all_to_all(jnp.broadcast_to(array[None], (size, *array.shape)), axis,...  15.1 us
    reduce_sum x2, other arithmetic, over_pieces(): return lax.all_gather(array, axis).sum(0)  13.3 us
    scatter-add x1, other arithmetic, local(): delta = jnp.zeros_like(table).at[received.reshape(-1)].add(arrived.reshap...  13.2 us
    unnamed x50, local copies, waits for them, and re-layouts  11.2 us
    all_to_all x1, starting transfers between devices, local(): lax.all_to_all(mine, 'dp', split_axis=1, concat_axis=1, tiled=True)  10.1 us
    all_to_all x1, waiting for transfers between devices, local(): lax.all_to_all(own_cot, 'dp', split_axis=1, concat_axis=1, tiled=True)  9.19 us
  transfers between devices with their start and end apart: 7, of which 6 were waited for; matrix products, arithmetic and copies ran while one was open for 13% of the time, Pallas kernels for 0%

commit v1 on v0

--- a/solution.py
+++ b/solution.py
@@ -63,7 +63,9 @@
     span = slots_all // lax.axis_size("mp")
     begin = lax.axis_index("mp") * span
     mine = lax.dynamic_slice_in_dim(hot_rows, begin, span, 2)
-    received = lax.all_to_all(mine, "dp", split_axis=1, concat_axis=1, tiled=True)
+    received = jnp.concatenate(
+        lax.all_to_all(jnp.stack(jnp.split(mine, lax.axis_size("dp"), axis=1)), "dp", 0, 0), axis=1
+    )
     fetched = jnp.take(table, received.reshape(-1), axis=0).astype(jnp.bfloat16)
     fetched = fetched.reshape(received.shape + (width,))
     returned = lax.all_to_all(fetched, "dp", split_axis=1, concat_axis=1, tiled=True)

time: 271 us -> 274 us (1.011)
  local copies, waits for them, and re-layouts: 16.5 us -> 51.5 us
  waiting for transfers between devices: 126 us -> 94.9 us
    unnamed x50 -> x116, local copies, waits for them, and re-layouts: 11.2 us -> 43.6 us
    all_gather x2, waiting for transfers between devices: 44.7 us -> 15.4 us  [over_pieces(): return lax.all_gather(array, axis).sum(0)]
    psum x1, waiting for transfers between devices: 54.9 us -> 50.2 us  [local(): lax.psum((part_one, part_two, part_three, part_four), 'dp')]
  transfers between devices with their start and end apart: 7 -> 7, of which waited for: 6 -> 6; matrix products, arithmetic and copies ran while one was open for 13% -> 25% of each run, Pallas kernels for 0% -> 0%
where the time goes in v1:
time: 274 us; the launch traced here: 273 us
  waiting for transfers between devices  94.9 us (35%)
  local copies, waits for them, and re-layouts  51.5 us (19%)
  other arithmetic  43.4 us (16%)
  matrix products  30.3 us (11%)
  starting transfers between devices  24.6 us (9%)
  blocking collectives  14.6 us (5%)
  between operations  14.1 us (5%)
    psum x1, waiting for transfers between devices, local(): lax.psum((part_one, part_two, part_three, part_four), 'dp')  50.2 us
    unnamed x116, local copies, waits for them, and re-layouts  43.6 us
    all_gather x2, waiting for transfers between devices, over_pieces(): return lax.all_gather(array, axis).sum(0)  15.4 us
    all_to_all x3, blocking collectives, from_everyone(): lax.all_to_all(jnp.broadcast_to(array[None], (size, *array.shape)), axis,...  14.6 us
    reduce_sum x2, other arithmetic, over_pieces(): return lax.all_gather(array, axis).sum(0)  13.3 us
    scatter-add x1, other arithmetic, local(): delta = jnp.zeros_like(table).at[received.reshape(-1)].add(arrived.reshap...  13.2 us
    all_to_all x1, waiting for transfers between devices, local(): lax.all_to_all(fetched, 'dp', split_axis=1, concat_axis=1, tiled=True)  10.6 us
    all_to_all x1, starting transfers between devices, local(): lax.all_to_all(jnp.stack(jnp.split(mine, lax.axis_size('dp'), axis=1)), '...  10.1 us
  transfers between devices with their start and end apart: 7, of which 6 were waited for; matrix products, arithmetic and copies ran while one was open for 25% of the time, Pallas kernels for 0%

profile of v1, /device:TPU:1, one launch (start us, length us, event | category | flops | bytes accessed | tf_op | source)
XLA Modules:
  0.0 273.3 jit_solution(14070160502204006496)
XLA Ops:
  7.2 4.8 %fusion.9 = f32[1024,512]{1,0:T(8,128)S(1)} fusion(bf16[1024,512]{1,0:T(8,128)(2,1)} %param.19, s32[1024]{0:T(1024)} %param.18, s32[1024]{0:T(1024)} %param.17, s32[1024]{0:T(1024)} %param.16), kind=kOutput, calls=%fused_computation.21 | convolution fusion | flops 1086324736 | bytes 3158016 | tf_op jit(solution)/shard_map/dot_general | solution.py:74
  12.0 1.3 copy-done.21
  13.4 3.3 %fusion.89 = f32[1024,1024]{1,0:T(8,128)} fusion(bf16[512,1024]{1,0:T(8,128)(2,1)S(1)} %copy-done.14, f32[1024,512]{1,0:T(8,128)S(1)} %fusion.9), kind=kOutput, calls=%fused_computation.241 | convolution fusion | flops 1076363264 | bytes 7340032 | tf_op jit(solution)/shard_map/dot_general | solution.py:76
  16.7 0.6 copy-done.2
  18.8 0.5 fusion.18
  19.3 0.5 constant_dynamic-update-slice_fusion.63
  19.9 0.5 constant_dynamic-update-slice_fusion.62
  20.4 0.5 constant_dynamic-update-slice_fusion.61
  20.9 0.5 constant_dynamic-update-slice_fusion.60
  21.4 0.5 constant_dynamic-update-slice_fusion.59
  21.9 0.5 constant_dynamic-update-slice_fusion.58
  22.4 0.5 constant_dynamic-update-slice_fusion.57
  22.9 0.5 constant_dynamic-update-slice_fusion.56
  23.4 0.5 constant_dynamic-update-slice_fusion.55
  24.0 0.5 constant_dynamic-update-slice_fusion.54
  28.0 15.0 %all-gather.5.cloned.1.call-done = f32[2048,1024]{1,0:T(8,128)} async-done(((f32[1024,1024]{1,0:T(8,128)}), f32[2048,1024]{1,0:T(8,128)}) %all-gather.5.cloned.1.call-update) | async-done | bytes 8388624 | tf_op jit(solution)/shard_map/all_gather | solution.py:12
  43.0 6.7 %reduce_sum.27 = f32[1024,1024]{1,0:T(8,128)} reduce(f32[2,1024,1024]{2,1,0:T(8,128)} %bitcast.170, f32[]{:T(128)} %constant.31.clone.1), dimensions={0}, to_apply=%region_1.2 | reduce | flops 1048576 | bytes 12582916 | tf_op jit(solution)/shard_map/reduce_sum | solution.py:12
  49.7 3.3 %multiply_convert_fusion.1 = bf16[1024,1024]{1,0:T(8,128)(2,1)S(1)} fusion(f32[1024,1024]{1,0:T(8,128)} %reduce_sum.27), kind=kLoop, calls=%fused_computation.8 | loop fusion | flops 5242880 | bytes 6291456 | tf_op jit(solution)/shard_map/convert_element_type | solution.py:77
  53.0 1.5 multiply_convert_fusion.4
  54.6 0.9 multiply_convert_fusion.3
  55.5 1.0 copy-done.19
  56.5 3.2 %fusion.91 = f32[1024,1024]{1,0:T(8,128)} fusion(bf16[1024,512]{1,0:T(8,128)(2,1)S(1)} %multiply_convert_fusion.3, bf16[1024,512]{1,0:T(8,128)(2,1)S(1)} %copy-done), kind=kOutput, calls=%fused_computation.245 | convolution fusion | flops 1073741824 | bytes 6291456 | tf_op jit(solution)/shard_map/dot_general | solution.py:95
  60.0 0.5 constant_dynamic-update-slice_fusion.46
  60.5 0.5 constant_dynamic-update-slice_fusion.45
  61.0 0.5 constant_dynamic-update-slice_fusion.44
  61.5 0.5 constant_dynamic-update-slice_fusion.43
  62.0 0.5 constant_dynamic-update-slice_fusion.42
  62.5 0.5 constant_dynamic-update-slice_fusion.41
  63.0 0.5 constant_dynamic-update-slice_fusion.40
  77.9 1.2 convolution_multiply_fusion.2
  79.1 4.2 %convolution_multiply_fusion = f32[1024,512]{1,0:T(8,128)} fusion(bf16[1024,1024]{1,0:T(8,128)(2,1)} %copy-done.6, bf16[1024,512]{1,0:T(8,128)(2,1)S(1)} %copy-done.20), kind=kOutput, calls=%fused_computation.23 | convolution fusion | flops 1074266112 | bytes 5242880 | tf_op jit(solution)/shard_map/dot_general | solution.py:97
  83.8 6.7 %reduce_sum.29 = f32[1024,1024]{1,0:T(8,128)} reduce(f32[2,1024,1024]{2,1,0:T(8,128)} %bitcast.171, f32[]{:T(128)} %constant.31.clone.1), dimensions={0}, to_apply=%region_3.4 | reduce | flops 1048576 | bytes 12582916 | tf_op jit(solution)/shard_map/reduce_sum | solution.py:12
  90.5 5.0 %multiply_convert_fusion = bf16[1024,1024]{1,0:T(8,128)(2,1)S(1)} fusion(f32[1024,1024]{1,0:T(8,128)} %reduce_sum.29, f32[1024,1024]{1,0:T(8,128)} %reduce_sum.27), kind=kLoop, calls=%fused_computation.7 | loop fusion | flops 9437184 | bytes 10485760 | tf_op jit(solution)/shard_map/convert_element_type | solution.py:98
  95.6 2.6 convolution_multiply_fusion.1
  98.2 8.1 %fusion.11 = f32[1024,512]{1,0:T(8,128)} fusion(s32[1024]{0:T(1024)S(1)} %copy-done.16, s32[1024]{0:T(1024)S(1)} %copy-done.17, s32[1024]{0:T(1024)S(1)} %copy-done.18, f32[1024,512]{1,0:T(8,128)} %copy-done.21, bf16[1024,1024]{1,0:T(8,128)(2,1)S(1)} %multiply_convert_fusion, bf16[512,1024]{1,0:T(8,128)(2,1)S(1)} %copy-done.15), kind=kOutput, calls=%fused_computation.25 | convolution fusion | flops 2165309440 | bytes 7352320 | tf_op jit(solution)/shard_map/dot_general | solution.py:103
  106.4 0.5 constant_dynamic-update-slice_fusion.11
  112.5 10.1 %all-to-all-start = ((s32[64,1,1,16]{3,2,1,0:T(1,128)}), s32[64,1,1,16]{3,2,1,0:T(1,128)S(1)}, u32[]{:S(2)}, u32[]{:S(2)}) async-start(s32[64,1,1,16]{3,2,1,0:T(1,128)} %constant_dynamic-update-slice_fusion), calls=%async_computation | async-start | bytes 65536 | tf_op jit(solution)/shard_map/all_to_all | solution.py:67
  122.7 8.7 %all-to-all-done = s32[64,1,1,16]{3,2,1,0:T(1,128)S(1)} async-done(((s32[64,1,1,16]{3,2,1,0:T(1,128)}), s32[64,1,1,16]{3,2,1,0:T(1,128)S(1)}, u32[]{:S(2)}, u32[]{:S(2)}) %all-to-all-start) | async-done | bytes 4128 | tf_op jit(solution)/shard_map/all_to_all | solution.py:67
  131.4 0.7 reshape.257
  132.1 4.8 %all-to-all-start.3 = ((s32[2,1,1024]{2,1,0:T(1,128)}), s32[2,1,1024]{2,1,0:T(1,128)S(1)}, u32[]{:S(2)}, u32[]{:S(2)}) async-start(s32[2,1,1024]{2,1,0:T(1,128)} %reshape.257), calls=%async_computation.3 | async-start | bytes 16384 | tf_op jit(solution)/shard_map/all_to_all | solution.py:17
  137.5 0.7 reduce.131
  138.3 2.9 %gather_fusion = bf16[1024,128]{1,0:T(8,128)(2,1)S(1)} fusion(f32[4096,128]{1,0:T(8,128)S(1)} %copy-done.3, s32[1024]{0:T(1024)S(1)} %broadcast_clamp_fusion), kind=kCustom, calls=%fused_computation | custom fusion | bytes 528384 | tf_op jit(solution)/shard_map/jit(_take)/gather | solution.py:69
  141.2 0.9 select_convert_fusion
  142.2 4.7 %all-to-all-start.1 = ((bf16[1,64,16,128]{3,2,0,1:T(8,128)(2,1)}), bf16[1,64,16,128]{3,2,0,1:T(8,128)(2,1)S(1)}, u32[]{:S(2)}, u32[]{:S(2)}) async-start(bf16[1,64,16,128]{3,2,0,1:T(8,128)(2,1)} %select_convert_fusion), calls=%async_computation.1 | async-start | bytes 524288 | tf_op jit(solution)/shard_map/all_to_all | solution.py:71
  146.9 0.5 broadcast.204
  147.4 0.7 reduce.132
  148.4 10.6 %all-to-all-done.1 = bf16[1,64,16,128]{3,2,0,1:T(8,128)(2,1)S(1)} async-done(((bf16[1,64,16,128]{3,2,0,1:T(8,128)(2,1)}), bf16[1,64,16,128]{3,2,0,1:T(8,128)(2,1)S(1)}, u32[]{:S(2)}, u32[]{:S(2)}) %all-to-all-start.1) | async-done | bytes 262176 | tf_op jit(solution)/shard_map/all_to_all | solution.py:71
  159.1 0.9 dynamic-slice_select_fusion
  160.0 4.9 %all_to_all.35 = bf16[2,1,64,16,128]{4,3,2,1,0:T(8,128)(2,1)S(1)} all-to-all(bf16[2,1,64,16,128]{4,3,2,1,0:T(8,128)(2,1)S(1)} %broadcast_in_dim.63), channel_id=1, replica_groups=mesh['dp'=64,'mp'=2] {'mp'}, dimensions={0} | all-to-all | bytes 1048576 | tf_op jit(solution)/shard_map/all_to_all | solution.py:17
  164.9 4.7 %all-to-all-start.4 = ((bf16[1,64,16,128]{3,2,0,1:T(8,128)(2,1)}), bf16[1,64,16,128]{3,2,0,1:T(8,128)(2,1)S(1)}, u32[]{:S(2)}, u32[]{:S(2)}) async-start(bf16[1,64,16,128]{3,2,0,1:T(8,128)(2,1)} %get-tuple-element.75), calls=%async_computation.4 | async-start | bytes 524288 | tf_op jit(solution)/shard_map/all_to_all | solution.py:88
  169.6 0.8 copy.231
  170.4 9.8 %all-to-all-done.4 = bf16[1,64,16,128]{3,2,0,1:T(8,128)(2,1)S(1)} async-done(((bf16[1,64,16,128]{3,2,0,1:T(8,128)(2,1)}), bf16[1,64,16,128]{3,2,0,1:T(8,128)(2,1)S(1)}, u32[]{:S(2)}, u32[]{:S(2)}) %all-to-all-start.4) | async-done | bytes 262176 | tf_op jit(solution)/shard_map/all_to_all | solution.py:88
  180.3 5.2 %all_to_all.36 = bf16[2,1,64,16,128]{4,3,2,1,0:T(8,128)(2,1)S(1)} all-to-all(bf16[2,1,64,16,128]{4,3,2,1,0:T(8,128)(2,1)S(1)} %broadcast_in_dim.67), channel_id=1, replica_groups=mesh['dp'=64,'mp'=2] {'mp'}, dimensions={0} | all-to-all | bytes 1048576 | tf_op jit(solution)/shard_map/all_to_all | solution.py:17
  185.5 1.1 copy_convert_fusion
  186.6 13.2 %scatter_custom_fusion = f32[4096,128]{1,0:T(8,128)} fusion(s32[2048]{0:T(1024)S(1)} %bitcast.180, f32[2048,128]{1,0:T(8,128)} %bitcast.174, f32[]{:T(128)} %constant.31.clone.1), kind=kCustom, calls=%fused_computation.27 | custom fusion | flops 262144 | bytes 2097664 | tf_op jit(solution)/shard_map/scatter-add | solution.py:113
  199.8 3.2 %multiply_subtract_fusion = f32[4096,128]{1,0:T(8,128)} fusion(f32[4096,128]{1,0:T(8,128)S(1)} %copy-done.3, f32[4096,128]{1,0:T(8,128)} %scatter_custom_fusion), kind=kLoop, calls=%fused_computation.22 | loop fusion | flops 1048576 | bytes 6291456 | tf_op jit(solution)/shard_map/sub | solution.py:115
  203.6 4.6 %all_to_all.37 = f32[2,1024,128]{2,1,0:T(8,128)S(1)} all-to-all(f32[2,1024,128]{2,1,0:T(8,128)S(1)} %broadcast_in_dim.68), channel_id=1, replica_groups=mesh['dp'=64,'mp'=2] {'mp'}, dimensions={0} | all-to-all | bytes 2097152 | tf_op jit(solution)/shard_map/all_to_all | solution.py:17
  208.1 0.8 reduce_sum.28
  208.9 50.2 %all-reduce.3.cloned.1.call-done = (f32[1024,512]{1,0:T(8,128)}, f32[512,1024]{1,0:T(8,128)}, f32[1024,512]{1,0:T(8,128)}, f32[512,128]{1,0:T(8,128)}) async-done(((f32[1024,512]{1,0:T(8,128)}, f32[512,1024]{1,0:T(8,128)}, f32[1024,512]{1,0:T(8,128)}, f32[512,128]{1,0:T(8,128)}), (f32[1024,512]{1,0:T(8,128)}, f32[512,1024]{1,0:T(8,128)}, f32[1024,512]{1,0:T(8,128)}, ...) | async-done | bytes 6553616 | tf_op jit(solution)/shard_map/psum | solution.py:104
  259.2 3.2 %copy.304 = f32[1024,512]{1,0:T(8,128)} copy(f32[1024,512]{1,0:T(8,128)} %get-tuple-element.82) | data formatting | bytes 4194304
  262.4 1.3 copy.305
  263.8 1.0 copy-done.7
  264.8 1.3 copy.306
  266.1 0.7 copy.307
  (117 shorter events, 27.7 us)
Async XLA Ops:
  7.2 45.8 %copy-start = (bf16[1024,512]{1,0:T(8,128)(2,1)S(1)}, bf16[1024,512]{1,0:T(8,128)(2,1)}, u32[]{:S(2)}) copy-start(bf16[1024,512]{1,0:T(8,128)(2,1)} %param.21) | copy-start | bytes 3145732
  7.2 6.2 %copy-start.14 = (bf16[512,1024]{1,0:T(8,128)(2,1)S(1)}, bf16[512,1024]{1,0:T(8,128)(2,1)}, u32[]{:S(2)}) copy-start(bf16[512,1024]{1,0:T(8,128)(2,1)} %param.20) | copy-start | bytes 3145732
  7.2 35.8 %all-gather.5.cloned.1.call-start = ((), (), s32[]{:S(2)}) async-start(), calls=%async_computation.7 | async-start | bytes 12582912 | tf_op jit(solution)/shard_map/all_gather | solution.py:12
  12.0 1.3 copy-start.21
  16.6 0.7 copy-start.2
  16.6 67.2 %all-gather.7.cloned.1.call-start = ((), (), s32[]{:S(2)}) async-start(), calls=%async_computation.8 | async-start | bytes 12582912 | tf_op jit(solution)/shard_map/all_gather | solution.py:12
  53.0 1.6 copy-start.6
  53.0 1.6 copy-start.10
  53.0 1.6 copy-start.12
  54.6 23.3 %copy-start.4 = (bf16[1024,512]{1,0:T(8,128)(2,1)}, bf16[1024,512]{1,0:T(8,128)(2,1)S(1)}, u32[]{:S(2)}) copy-start(bf16[1024,512]{1,0:T(8,128)(2,1)S(1)} %get-tuple-element.77) | copy-start | bytes 3145732
  55.5 1.0 copy-start.19
  59.7 19.4 %copy-start.20 = (bf16[1024,512]{1,0:T(8,128)(2,1)S(1)}, bf16[1024,512]{1,0:T(8,128)(2,1)}, u32[]{:S(2)}) copy-start(bf16[1024,512]{1,0:T(8,128)(2,1)} %copy-done.19) | copy-start | bytes 3145732
  59.7 199.5 %all-reduce.3.cloned.1.call-start = ((), (), s32[]{:S(2)}) async-start(), calls=%async_computation.9 | async-start | bytes 13107200 | tf_op jit(solution)/shard_map/psum | solution.py:104
  90.5 5.1 %copy-start.22 = (f32[1024,512]{1,0:T(8,128)S(1)}, f32[1024,512]{1,0:T(8,128)}, u32[]{:S(2)}) copy-start(f32[1024,512]{1,0:T(8,128)} %copy-done.21) | copy-start | bytes 6291460
  95.5 2.7 copy-start.15
  95.5 2.7 copy-start.16
  95.6 2.7 copy-start.17
  95.6 2.7 copy-start.18
  106.3 32.0 %copy-start.3 = (f32[4096,128]{1,0:T(8,128)S(1)}, f32[4096,128]{1,0:T(8,128)}, u32[]{:S(2)}) copy-start(f32[4096,128]{1,0:T(8,128)} %param.15) | copy-start | bytes 6291460
  106.4 40.4 %copy-start.13 = (s32[1,64]{1,0:T(1,128)S(1)}, s32[1,64]{1,0:T(1,128)}, u32[]{:S(2)}) copy-start(s32[1,64]{1,0:T(1,128)} %param.13) | copy-start | bytes 772
  106.4 52.7 %copy-start.11 = (bf16[1,64,32,128]{3,2,1,0:T(8,128)(2,1)S(1)}, bf16[1,64,32,128]{3,2,1,0:T(8,128)(2,1)}, u32[]{:S(2)}) copy-start(bf16[1,64,32,128]{3,2,1,0:T(8,128)(2,1)} %param.14) | copy-start | bytes 1572868
  112.5 18.8 %all-to-all-start = ((s32[64,1,1,16]{3,2,1,0:T(1,128)}), s32[64,1,1,16]{3,2,1,0:T(1,128)S(1)}, u32[]{:S(2)}, u32[]{:S(2)}) async-start(s32[64,1,1,16]{3,2,1,0:T(1,128)} %constant_dynamic-update-slice_fusion), calls=%async_computation | async-start | bytes 65536 | tf_op jit(solution)/shard_map/all_to_all | solution.py:67
  132.1 10.0 %all-to-all-start.3 = ((s32[2,1,1024]{2,1,0:T(1,128)}), s32[2,1,1024]{2,1,0:T(1,128)S(1)}, u32[]{:S(2)}, u32[]{:S(2)}) async-start(s32[2,1,1024]{2,1,0:T(1,128)} %reshape.257), calls=%async_computation.3 | async-start | bytes 16384 | tf_op jit(solution)/shard_map/all_to_all | solution.py:17
  142.2 16.9 %all-to-all-start.1 = ((bf16[1,64,16,128]{3,2,0,1:T(8,128)(2,1)}), bf16[1,64,16,128]{3,2,0,1:T(8,128)(2,1)S(1)}, u32[]{:S(2)}, u32[]{:S(2)}) async-start(bf16[1,64,16,128]{3,2,0,1:T(8,128)(2,1)} %select_convert_fusion), calls=%async_computation.1 | async-start | bytes 524288 | tf_op jit(solution)/shard_map/all_to_all | solution.py:71
  164.9 15.4 %all-to-all-start.4 = ((bf16[1,64,16,128]{3,2,0,1:T(8,128)(2,1)}), bf16[1,64,16,128]{3,2,0,1:T(8,128)(2,1)S(1)}, u32[]{:S(2)}, u32[]{:S(2)}) async-start(bf16[1,64,16,128]{3,2,0,1:T(8,128)(2,1)} %get-tuple-element.75), calls=%async_computation.4 | async-start | bytes 524288 | tf_op jit(solution)/shard_map/all_to_all | solution.py:88
  199.8 3.2 %copy-start.5 = (bf16[1024,512]{1,0:T(8,128)(2,1)S(1)}, bf16[1024,512]{1,0:T(8,128)(2,1)}, u32[]{:S(2)}) copy-start(bf16[1024,512]{1,0:T(8,128)(2,1)} %copy-done.4) | copy-start | bytes 3145732
  259.2 3.2 %copy-start.8 = (f32[512,1024]{1,0:T(8,128)S(1)}, f32[512,1024]{1,0:T(8,128)}, u32[]{:S(2)}) copy-start(f32[512,1024]{1,0:T(8,128)} %get-tuple-element.83) | copy-start | bytes 6291460
  262.4 2.3 copy-start.7
  262.4 4.4 %copy-start.1 = (bf16[1024,512]{1,0:T(8,128)(2,1)S(1)}, bf16[1024,512]{1,0:T(8,128)(2,1)}, u32[]{:S(2)}) copy-start(bf16[1024,512]{1,0:T(8,128)(2,1)} %param.21) | copy-start | bytes 3145732
  264.8 1.3 copy-start.9
Sparse Core Ops, SparseCore 0:
  16.8 26.1 all-gather.4
  59.9 23.8 all-gather.6
  106.5 152.6 all-reduce.2
